TPU v7x, 1024 devices: a whole 4x8x16 slice. The times are simulated.
1024 devices in a mesh: ctx: 128 (over z, y), head: 8 (over x, core).
Axes of the slice: x: 4, y: 8, z: 16, core: 2. Of those that a mesh axis runs over, the one named last changes fastest.
Arguments:
- queries: bfloat16 [65536, 4096], P('ctx', 'head'), may hold values from -8 to 8
- keys: bfloat16 [65536, 1024], P('ctx', 'head'), may hold values from -8 to 8
- values: bfloat16 [65536, 1024], P('ctx', 'head'), may hold values from -6 to 6
- output_gradient: bfloat16 [65536, 4096], P('ctx', 'head'), may hold values from -6 to 6
- blocks: int32 [512, 8], P('ctx'), may hold values from 0 to 511, as said below
- counts: int32 [512], P('ctx'), may hold values from 2 to 8, as said below
Outputs:
- dqueries: bfloat16 [65536, 4096], P(('ctx', 'head'))
- dkeys: bfloat16 [65536, 1024], P(('ctx', 'head'))
- dvalues: bfloat16 [65536, 1024], P(('ctx', 'head'))
Inputs may be any that keep to these rules, and one draw needn't show every extreme that they name: For the query block b on token shard i = b // 4, all 8 entries of row b are distinct and name key blocks of the shards i - 2 to i + 2, taken around the closed cycle of 512 blocks. `counts`: some rows have all 8 entries live.
All inputs are finite; a program needn't handle non-finite values.
Results may differ from a plain program's by a relative error of at most 0.0088.
Values may be sent and summed in bfloat16 or wider, within the bound.
A program may use at most 32 MiB of HBM per device.

v0:
```python
import math

import jax
import jax.numpy as jnp
from jax import lax
from jax.sharding import PartitionSpec as P

HEAD_SIZE = 128
BLOCK_TOKENS = 128
SLOTS = 8
REACH = 2


def from_behind(x, axis, by):
    size = lax.axis_size(axis)
    return lax.ppermute(x, axis, [(i, (i + by) % size) for i in range(size)])


def send_back(segment, shift_by):
    return from_behind(segment, "ctx", shift_by)


def kv_neighbour(piece, offset):
    return from_behind(piece, "ctx", -offset)


def collect_window(piece, axis_dim, fetcher):
    pieces = []
    for offset in range(-REACH, REACH + 1):
        if offset == 0:
            pieces.append(piece)
        else:
            pieces.append(fetcher(piece, offset))
    return jnp.concatenate(pieces, axis=axis_dim)


def on_device(queries, keys, values, output_gradient, blocks, counts):
    tok_rows, query_width = queries.shape
    kv_width = keys.shape[1]
    kv_heads = kv_width // HEAD_SIZE
    query_group = query_width // kv_width
    own_blocks = tok_rows // BLOCK_TOKENS
    cycle_size = lax.axis_size("ctx")
    my_index = lax.axis_index("ctx")
    softmax_scale = 1.0 / math.sqrt(HEAD_SIZE)
    stacked = jnp.stack([keys, values])
    extended = collect_window(stacked, 1, kv_neighbour)
    window_blocks = (2 * REACH + 1) * own_blocks
    extended = extended.reshape(2, window_blocks, BLOCK_TOKENS, kv_heads, HEAD_SIZE)
    first_block = (my_index - REACH) * own_blocks
    local_blocks = jnp.mod(blocks - first_block, cycle_size * own_blocks)
    blocked_queries = queries.reshape(own_blocks, BLOCK_TOKENS, kv_heads, query_group, HEAD_SIZE)
    output_blocks = output_gradient.reshape(
        own_blocks, BLOCK_TOKENS, kv_heads, query_group, HEAD_SIZE
    )

    def one_block(qblock, running):
        gradients, dquery_blocks, stat_blocks = running
        slot_blocks = local_blocks[qblock]
        live_slots = jnp.arange(SLOTS) < counts[qblock]
        live_mask = live_slots[None, None, None, :, None]
        kblock = extended[0][slot_blocks]
        vblock = extended[1][slot_blocks]
        qrows = blocked_queries[qblock]
        orows = output_blocks[qblock]
        scores = (
            jnp.einsum("rhgd,schd->hgrsc", qrows, kblock, preferred_element_type=jnp.float32)
            * softmax_scale
        )
        scores = jnp.where(live_mask, scores, -1e30)
        row_max = jnp.max(scores, axis=(3, 4), keepdims=True)
        weights = jnp.where(live_mask, jnp.exp(scores - row_max), 0.0)
        total = jnp.sum(weights, axis=(3, 4), keepdims=True)
        probs = weights / total
        dprobs = jnp.einsum("rhgd,schd->hgrsc", orows, vblock, preferred_element_type=jnp.float32)
        row_delta = jnp.sum(probs * dprobs, axis=(3, 4), keepdims=True)
        dscores = (probs * (dprobs - row_delta)).astype(jnp.bfloat16)
        dquery = softmax_scale * jnp.einsum(
            "hgrsc,schd->rhgd", dscores, kblock, preferred_element_type=jnp.float32
        )
        dquery_blocks = dquery_blocks.at[qblock].set(dquery.astype(jnp.bfloat16))
        probs_bf = probs.astype(jnp.bfloat16)
        dkey_part = softmax_scale * jnp.einsum(
            "hgrsc,rhgd->schd", dscores, qrows, preferred_element_type=jnp.float32
        )
        dvalue_part = jnp.einsum(
            "hgrsc,rhgd->schd", probs_bf, orows, preferred_element_type=jnp.float32
        )
        gradients = gradients.at[0, slot_blocks].add(dkey_part)
        gradients = gradients.at[1, slot_blocks].add(dvalue_part)
        return (gradients, dquery_blocks, stat_blocks)

    start_grads = jnp.zeros((2, window_blocks, BLOCK_TOKENS, kv_heads, HEAD_SIZE), jnp.float32)
    start_dquery = jnp.zeros(
        (own_blocks, BLOCK_TOKENS, kv_heads, query_group, HEAD_SIZE), jnp.bfloat16
    )
    start_stats = jnp.zeros((2, own_blocks, BLOCK_TOKENS, kv_heads, query_group), jnp.float32)
    gradients, dquery_blocks, stat_blocks = lax.fori_loop(
        0, own_blocks, one_block, (start_grads, start_dquery, start_stats)
    )
    segments = gradients.reshape(2, 2 * REACH + 1, tok_rows, kv_width)
    summed = segments[:, REACH]
    for offset in range(1, REACH + 1):
        for direction in (1, -1):
            summed = summed + send_back(segments[:, REACH + direction * offset], direction * offset)
    dkeys = summed[0].astype(jnp.bfloat16)
    dvalues = summed[1].astype(jnp.bfloat16)
    dqueries = dquery_blocks.reshape(tok_rows, query_width)
    return (
        lax.all_to_all(dqueries, "head", split_axis=0, concat_axis=1, tiled=True),
        lax.all_to_all(dkeys, "head", split_axis=0, concat_axis=1, tiled=True),
        lax.all_to_all(dvalues, "head", split_axis=0, concat_axis=1, tiled=True),
    )


def solution(mesh):
    return jax.shard_map(
        on_device,
        mesh=mesh,
        in_specs=(
            P("ctx", "head"),
            P("ctx", "head"),
            P("ctx", "head"),
            P("ctx", "head"),
            P("ctx", None),
            P("ctx"),
        ),
        out_specs=(P(("ctx", "head"), None), P(("ctx", "head"), None), P(("ctx", "head"), None)),
        check_vma=False,
    )
```

profile of v0, /device:TPU:1, one launch (start us, length us, event | category | flops | bytes accessed | tf_op | source)
XLA Modules:
  0.0 196.9 jit_solution(11238478630633171104)
XLA Ops:
  1.7 5.0 %collective-permute-start = (bf16[2,512,128]{2,1,0:T(8,128)(2,1)S(1)}, bf16[2,512,128]{2,1,0:T(8,128)(2,1)S(1)}, u32[]{:S(2)}, u32[]{:S(2)}) collective-permute-start(bf16[2,512,128]{2,1,0:T(8,128)(2,1)S(1)} %pad_maximum_fusion), channel_id=1, source_target_pairs={{0,16},{8,24},{16,32},{24,40},{32,48},{40,56},{48,64},{56,72},{64,... | collective-permute-start | bytes 786440 | tf_op jit(solution)/shard_map/ppermute | solution.py:16
  6.8 3.2 %collective-permute-start.1 = (bf16[2,512,128]{2,1,0:T(8,128)(2,1)S(1)}, bf16[2,512,128]{2,1,0:T(8,128)(2,1)S(1)}, u32[]{:S(2)}, u32[]{:S(2)}) collective-permute-start(bf16[2,512,128]{2,1,0:T(8,128)(2,1)S(1)} %pad_maximum_fusion), channel_id=1, source_target_pairs={{0,8},{8,16},{16,24},{24,32},{32,40},{40,48},{48,56},{56,64},{64,7... | collective-permute-start | bytes 786440 | tf_op jit(solution)/shard_map/ppermute | solution.py:16
  10.0 17.3 %collective-permute-start.2 = (bf16[2,512,128]{2,1,0:T(8,128)(2,1)S(1)}, bf16[2,512,128]{2,1,0:T(8,128)(2,1)S(1)}, u32[]{:S(2)}, u32[]{:S(2)}) collective-permute-start(bf16[2,512,128]{2,1,0:T(8,128)(2,1)S(1)} %pad_maximum_fusion), channel_id=1, source_target_pairs={{0,1016},{8,0},{16,8},{24,16},{32,24},{40,32},{48,40},{56,48},{64,... | collective-permute-start | bytes 786440 | tf_op jit(solution)/shard_map/ppermute | solution.py:16
  27.3 4.3 %collective-permute-start.3 = (bf16[2,512,128]{2,1,0:T(8,128)(2,1)S(1)}, bf16[2,512,128]{2,1,0:T(8,128)(2,1)S(1)}, u32[]{:S(2)}, u32[]{:S(2)}) collective-permute-start(bf16[2,512,128]{2,1,0:T(8,128)(2,1)S(1)} %pad_maximum_fusion), channel_id=1, source_target_pairs={{0,1008},{8,1016},{16,0},{24,8},{32,16},{40,24},{48,32},{56,40},{6... | collective-permute-start | bytes 786440 | tf_op jit(solution)/shard_map/ppermute | solution.py:16
  35.8 4.8 %collective-permute-done.1 = bf16[2,512,128]{2,1,0:T(8,128)(2,1)S(1)} collective-permute-done((bf16[2,512,128]{2,1,0:T(8,128)(2,1)S(1)}, bf16[2,512,128]{2,1,0:T(8,128)(2,1)S(1)}, u32[]{:S(2)}, u32[]{:S(2)}) %collective-permute-start.1) | collective-permute-done | bytes 262176 | tf_op jit(solution)/shard_map/ppermute | solution.py:16
  43.5 1.8 broadcast_in_dim.63
  46.2 83.0 %while.16 = (s32[]{:T(128)}, f32[2,20,128,1,128]{4,2,1,0,3:T(8,128)}, bf16[4,128,1,4,128]{4,3,1,0,2:T(4,128)(2,1)}, s32[4,8]{1,0:T(4,128)S(1)}, bf16[4,128,1,4,1...) while((s32[]{:T(128)}, ...), condition=%wide.region_7.8_spmd, body=%wide.region_0.7_spmd.sunk | while | flops 686882432 | bytes 41464688 | solution.py:98
  51.1 1.6 convolution_bitcast_fusion.4
  52.7 2.1 %copy.104 = f32[8,128,128]{2,1,0:T(8,128)} copy(f32[8,128,128]{1,2,0:T(8,128)} %convolution_bitcast_fusion.4) | data formatting | bytes 1048576 | tf_op jit(solution)/shard_map/while/body/eval_jaxpr/hgrsc,rhgd->schd/transpose | solution.py:86
  57.8 2.7 %scatter_fusion = f32[2,20,128,128]{3,2,1,0:T(8,128)} fusion(f32[2,20,128,128]{3,2,1,0:T(8,128)} %bitcast.277, s32[8]{0:T(128)S(1)} %select_bitcast_fusion.5, f32[8,128,128]{2,1,0:T(8,128)S(1)} %copy.103), kind=kCustom, calls=%fused_computation.2.clone.1 | custom fusion | flops 131072 | bytes 1572928 | tf_op jit(solution)/shard_map/while/body/eval_jaxpr/scatter-add | solution.py:89
  60.5 2.7 %scatter_fusion.1 = f32[2,20,128,128]{3,2,1,0:T(8,128)} fusion(f32[2,20,128,128]{3,2,1,0:T(8,128)} %scatter_fusion, s32[8]{0:T(128)S(1)} %get-tuple-element.283, f32[8,128,128]{2,1,0:T(8,128)S(1)} %copy-done), kind=kCustom, calls=%fused_computation.3.clone.1 | custom fusion | flops 131072 | bytes 1572928 | tf_op jit(solution)/shard_map/while/body/eval_jaxpr/scatter-add | solution.py:90
  73.5 2.1 %copy.104 = f32[8,128,128]{2,1,0:T(8,128)} copy(f32[8,128,128]{1,2,0:T(8,128)} %convolution_bitcast_fusion.4) | data formatting | bytes 1048576 | tf_op jit(solution)/shard_map/while/body/eval_jaxpr/hgrsc,rhgd->schd/transpose | solution.py:86
  78.5 2.7 %scatter_fusion = f32[2,20,128,128]{3,2,1,0:T(8,128)} fusion(f32[2,20,128,128]{3,2,1,0:T(8,128)} %bitcast.277, s32[8]{0:T(128)S(1)} %select_bitcast_fusion.5, f32[8,128,128]{2,1,0:T(8,128)S(1)} %copy.103), kind=kCustom, calls=%fused_computation.2.clone.1 | custom fusion | flops 131072 | bytes 1572928 | tf_op jit(solution)/shard_map/while/body/eval_jaxpr/scatter-add | solution.py:89
  81.3 2.8 %scatter_fusion.1 = f32[2,20,128,128]{3,2,1,0:T(8,128)} fusion(f32[2,20,128,128]{3,2,1,0:T(8,128)} %scatter_fusion, s32[8]{0:T(128)S(1)} %get-tuple-element.283, f32[8,128,128]{2,1,0:T(8,128)S(1)} %copy-done), kind=kCustom, calls=%fused_computation.3.clone.1 | custom fusion | flops 131072 | bytes 1572928 | tf_op jit(solution)/shard_map/while/body/eval_jaxpr/scatter-add | solution.py:90
  92.7 1.6 convolution_bitcast_fusion.4
  94.3 2.1 %copy.104 = f32[8,128,128]{2,1,0:T(8,128)} copy(f32[8,128,128]{1,2,0:T(8,128)} %convolution_bitcast_fusion.4) | data formatting | bytes 1048576 | tf_op jit(solution)/shard_map/while/body/eval_jaxpr/hgrsc,rhgd->schd/transpose | solution.py:86
  99.3 2.7 %scatter_fusion = f32[2,20,128,128]{3,2,1,0:T(8,128)} fusion(f32[2,20,128,128]{3,2,1,0:T(8,128)} %bitcast.277, s32[8]{0:T(128)S(1)} %select_bitcast_fusion.5, f32[8,128,128]{2,1,0:T(8,128)S(1)} %copy.103), kind=kCustom, calls=%fused_computation.2.clone.1 | custom fusion | flops 131072 | bytes 1572928 | tf_op jit(solution)/shard_map/while/body/eval_jaxpr/scatter-add | solution.py:89
  102.1 2.7 %scatter_fusion.1 = f32[2,20,128,128]{3,2,1,0:T(8,128)} fusion(f32[2,20,128,128]{3,2,1,0:T(8,128)} %scatter_fusion, s32[8]{0:T(128)S(1)} %get-tuple-element.283, f32[8,128,128]{2,1,0:T(8,128)S(1)} %copy-done), kind=kCustom, calls=%fused_computation.3.clone.1 | custom fusion | flops 131072 | bytes 1572928 | tf_op jit(solution)/shard_map/while/body/eval_jaxpr/scatter-add | solution.py:90
  115.0 2.1 %copy.104 = f32[8,128,128]{2,1,0:T(8,128)} copy(f32[8,128,128]{1,2,0:T(8,128)} %convolution_bitcast_fusion.4) | data formatting | bytes 1048576 | tf_op jit(solution)/shard_map/while/body/eval_jaxpr/hgrsc,rhgd->schd/transpose | solution.py:86
  120.1 2.7 %scatter_fusion = f32[2,20,128,128]{3,2,1,0:T(8,128)} fusion(f32[2,20,128,128]{3,2,1,0:T(8,128)} %bitcast.277, s32[8]{0:T(128)S(1)} %select_bitcast_fusion.5, f32[8,128,128]{2,1,0:T(8,128)S(1)} %copy.103), kind=kCustom, calls=%fused_computation.2.clone.1 | custom fusion | flops 131072 | bytes 1572928 | tf_op jit(solution)/shard_map/while/body/eval_jaxpr/scatter-add | solution.py:89
  122.8 2.7 %scatter_fusion.1 = f32[2,20,128,128]{3,2,1,0:T(8,128)} fusion(f32[2,20,128,128]{3,2,1,0:T(8,128)} %scatter_fusion, s32[8]{0:T(128)S(1)} %get-tuple-element.283, f32[8,128,128]{2,1,0:T(8,128)S(1)} %copy-done), kind=kCustom, calls=%fused_computation.3.clone.1 | custom fusion | flops 131072 | bytes 1572928 | tf_op jit(solution)/shard_map/while/body/eval_jaxpr/scatter-add | solution.py:90
  129.2 2.8 %slice_bitcast_fusion.5 = (f32[2,512,128]{2,1,0:T(8,128)}, f32[2,512,128]{2,1,0:T(8,128)}, f32[2,512,128]{2,1,0:T(8,128)S(1)}, f32[2,512,128]{2,1,0:T(8,128)}) fusion(f32[2,5,512,128]{3,2,1,0:T(8,128)} %bitcast.279), kind=kLoop, calls=%fused_computation.57 | loop fusion | bytes 4194304 | tf_op jit(solution)/shard_map/squeeze | solution.py:105
  132.0 1.9 collective-permute-start.4
  133.9 6.7 %collective-permute-start.5 = (f32[2,512,128]{2,1,0:T(8,128)}, f32[2,512,128]{2,1,0:T(8,128)S(1)}, u32[]{:S(2)}, u32[]{:S(2)}) collective-permute-start(f32[2,512,128]{2,1,0:T(8,128)} %get-tuple-element.210), channel_id=1, source_target_pairs={{0,1016},{8,0},{16,8},{24,16},{32,24},{40,32},{48,40},{56,48},{64,... | collective-permute-start | bytes 1572872 | tf_op jit(solution)/shard_map/ppermute | solution.py:16
  140.6 1.9 collective-permute-start.6
  142.5 7.6 %collective-permute-start.7 = (f32[2,512,128]{2,1,0:T(8,128)S(1)}, f32[2,512,128]{2,1,0:T(8,128)S(1)}, u32[]{:S(2)}, u32[]{:S(2)}) collective-permute-start(f32[2,512,128]{2,1,0:T(8,128)S(1)} %get-tuple-element.211), channel_id=1, source_target_pairs={{0,1008},{8,1016},{16,0},{24,8},{32,16},{40,24},{48,32},{56,40},{6... | collective-permute-start | bytes 1572872 | tf_op jit(solution)/shard_map/ppermute | solution.py:16
  151.1 7.1 %all-to-all-start = ((bf16[8,64,512]{2,1,0:T(8,128)(2,1)}), bf16[8,64,512]{2,1,0:T(8,128)(2,1)S(1)}, u32[]{:S(2)}, u32[]{:S(2)}) async-start(bf16[8,64,512]{2,1,0:T(8,128)(2,1)} %all_to_all.38), calls=%async_computation | async-start | bytes 1048576 | tf_op jit(solution)/shard_map/all_to_all | solution.py:110
  158.3 13.2 %collective-permute-done.5 = f32[2,512,128]{2,1,0:T(8,128)S(1)} collective-permute-done((f32[2,512,128]{2,1,0:T(8,128)}, f32[2,512,128]{2,1,0:T(8,128)S(1)}, u32[]{:S(2)}, u32[]{:S(2)}) %collective-permute-start.5) | collective-permute-done | bytes 524320 | tf_op jit(solution)/shard_map/ppermute | solution.py:16
  174.6 6.9 %all-to-all-start.2 = ((bf16[8,64,128]{2,1,0:T(8,128)(2,1)}), bf16[8,64,128]{2,1,0:T(8,128)(2,1)S(1)}, u32[]{:S(2)}, u32[]{:S(2)}) async-start(bf16[8,64,128]{2,1,0:T(8,128)(2,1)} %bitcast.56), calls=%async_computation.2 | async-start | bytes 262144 | tf_op jit(solution)/shard_map/all_to_all | solution.py:112
  182.4 4.4 %all-to-all-done.2 = bf16[8,64,128]{2,1,0:T(8,128)(2,1)S(1)} async-done(((bf16[8,64,128]{2,1,0:T(8,128)(2,1)}), bf16[8,64,128]{2,1,0:T(8,128)(2,1)S(1)}, u32[]{:S(2)}, u32[]{:S(2)}) %all-to-all-start.2) | async-done | bytes 131104 | tf_op jit(solution)/shard_map/all_to_all | solution.py:112
  186.8 4.1 %all-to-all-start.1 = ((bf16[8,64,128]{2,1,0:T(8,128)(2,1)}), bf16[8,64,128]{2,1,0:T(8,128)(2,1)S(1)}, u32[]{:S(2)}, u32[]{:S(2)}) async-start(bf16[8,64,128]{2,1,0:T(8,128)(2,1)} %bitcast.54), calls=%async_computation.1 | async-start | bytes 262144 | tf_op jit(solution)/shard_map/all_to_all | solution.py:111
  191.6 4.6 %all-to-all-done.1 = bf16[8,64,128]{2,1,0:T(8,128)(2,1)S(1)} async-done(((bf16[8,64,128]{2,1,0:T(8,128)(2,1)}), bf16[8,64,128]{2,1,0:T(8,128)(2,1)S(1)}, u32[]{:S(2)}, u32[]{:S(2)}) %all-to-all-start.1) | async-done | bytes 131104 | tf_op jit(solution)/shard_map/all_to_all | solution.py:111
  (219 shorter events, 64.3 us)
Async XLA Ops:
  0.6 40.7 %copy-start.7 = (bf16[512,128]{1,0:T(8,128)(2,1)S(1)}, bf16[512,128]{1,0:T(8,128)(2,1)}, u32[]{:S(2)}) copy-start(bf16[512,128]{1,0:T(8,128)(2,1)} %param.11) | copy-start | bytes 393220
  0.6 40.7 %copy-start.6 = (bf16[512,128]{1,0:T(8,128)(2,1)S(1)}, bf16[512,128]{1,0:T(8,128)(2,1)}, u32[]{:S(2)}) copy-start(bf16[512,128]{1,0:T(8,128)(2,1)} %param.12) | copy-start | bytes 393220
  0.7 33.2 %copy-start.13 = (s32[4,8]{1,0:T(4,128)S(1)}, s32[4,8]{1,0:T(4,128)}, u32[]{:S(2)}) copy-start(s32[4,8]{1,0:T(4,128)} %param.14) | copy-start | bytes 388
  1.7 33.3 %collective-permute-start = (bf16[2,512,128]{2,1,0:T(8,128)(2,1)S(1)}, bf16[2,512,128]{2,1,0:T(8,128)(2,1)S(1)}, u32[]{:S(2)}, u32[]{:S(2)}) collective-permute-start(bf16[2,512,128]{2,1,0:T(8,128)(2,1)S(1)} %pad_maximum_fusion), channel_id=1, source_target_pairs={{0,16},{8,24},{16,32},{24,40},{32,48},{40,56},{48,64},{56,72},{64,... | collective-permute-start | bytes 786440 | tf_op jit(solution)/shard_map/ppermute | solution.py:16
  6.8 33.8 %collective-permute-start.1 = (bf16[2,512,128]{2,1,0:T(8,128)(2,1)S(1)}, bf16[2,512,128]{2,1,0:T(8,128)(2,1)S(1)}, u32[]{:S(2)}, u32[]{:S(2)}) collective-permute-start(bf16[2,512,128]{2,1,0:T(8,128)(2,1)S(1)} %pad_maximum_fusion), channel_id=1, source_target_pairs={{0,8},{8,16},{16,24},{24,32},{32,40},{40,48},{48,56},{56,64},{64,7... | collective-permute-start | bytes 786440 | tf_op jit(solution)/shard_map/ppermute | solution.py:16
  10.0 32.1 %collective-permute-start.2 = (bf16[2,512,128]{2,1,0:T(8,128)(2,1)S(1)}, bf16[2,512,128]{2,1,0:T(8,128)(2,1)S(1)}, u32[]{:S(2)}, u32[]{:S(2)}) collective-permute-start(bf16[2,512,128]{2,1,0:T(8,128)(2,1)S(1)} %pad_maximum_fusion), channel_id=1, source_target_pairs={{0,1016},{8,0},{16,8},{24,16},{32,24},{40,32},{48,40},{56,48},{64,... | collective-permute-start | bytes 786440 | tf_op jit(solution)/shard_map/ppermute | solution.py:16
  27.3 15.5 %collective-permute-start.3 = (bf16[2,512,128]{2,1,0:T(8,128)(2,1)S(1)}, bf16[2,512,128]{2,1,0:T(8,128)(2,1)S(1)}, u32[]{:S(2)}, u32[]{:S(2)}) collective-permute-start(bf16[2,512,128]{2,1,0:T(8,128)(2,1)S(1)} %pad_maximum_fusion), channel_id=1, source_target_pairs={{0,1008},{8,1016},{16,0},{24,8},{32,16},{40,24},{48,32},{56,40},{6... | collective-permute-start | bytes 786440 | tf_op jit(solution)/shard_map/ppermute | solution.py:16
  42.0 4.2 %copy-start.14 = (s32[4]{0:T(128)S(1)}, s32[4]{0:T(128)}, u32[]{:S(2)}) copy-start(s32[4]{0:T(128)} %param.15) | copy-start | bytes 52
  57.6 5.8 %copy-start.16 = (s32[5]{0:T(128)S(1)}, s32[5]{0:T(128)}, u32[]{:S(2)}) copy-start(s32[5]{0:T(128)} %get-tuple-element.315) | copy-start | bytes 64 | tf_op jit(solution)/shard_map/while
  60.5 6.4 %copy-start.5 = (bf16[4,128,1,4,128]{4,3,1,0,2:T(4,128)(2,1)S(1)}, bf16[4,128,1,4,128]{4,3,1,0,2:T(4,128)(2,1)}, u32[]{:S(2)}) copy-start(bf16[4,128,1,4,128]{4,3,1,0,2:T(4,128)(2,1)} %copy-done.4) | copy-start | bytes 1572868 | tf_op jit(solution)/shard_map/while
  60.5 6.4 %copy-start.12 = (s32[4,8]{1,0:T(4,128)S(1)}, s32[4,8]{1,0:T(4,128)}, u32[]{:S(2)}) copy-start(s32[4,8]{1,0:T(4,128)} %copy-done.11) | copy-start | bytes 388 | tf_op jit(solution)/shard_map/while
  60.5 6.4 %copy-start.15 = (s32[4]{0:T(128)S(1)}, s32[4]{0:T(128)}, u32[]{:S(2)}) copy-start(s32[4]{0:T(128)} %get-tuple-element.344) | copy-start | bytes 52 | tf_op jit(solution)/shard_map/while
  78.3 5.9 %copy-start.16 = (s32[5]{0:T(128)S(1)}, s32[5]{0:T(128)}, u32[]{:S(2)}) copy-start(s32[5]{0:T(128)} %get-tuple-element.315) | copy-start | bytes 64 | tf_op jit(solution)/shard_map/while
  81.3 6.5 %copy-start.5 = (bf16[4,128,1,4,128]{4,3,1,0,2:T(4,128)(2,1)S(1)}, bf16[4,128,1,4,128]{4,3,1,0,2:T(4,128)(2,1)}, u32[]{:S(2)}) copy-start(bf16[4,128,1,4,128]{4,3,1,0,2:T(4,128)(2,1)} %copy-done.4) | copy-start | bytes 1572868 | tf_op jit(solution)/shard_map/while
  81.3 6.5 %copy-start.12 = (s32[4,8]{1,0:T(4,128)S(1)}, s32[4,8]{1,0:T(4,128)}, u32[]{:S(2)}) copy-start(s32[4,8]{1,0:T(4,128)} %copy-done.11) | copy-start | bytes 388 | tf_op jit(solution)/shard_map/while
  81.3 6.5 %copy-start.15 = (s32[4]{0:T(128)S(1)}, s32[4]{0:T(128)}, u32[]{:S(2)}) copy-start(s32[4]{0:T(128)} %get-tuple-element.344) | copy-start | bytes 52 | tf_op jit(solution)/shard_map/while
  99.1 5.8 %copy-start.16 = (s32[5]{0:T(128)S(1)}, s32[5]{0:T(128)}, u32[]{:S(2)}) copy-start(s32[5]{0:T(128)} %get-tuple-element.315) | copy-start | bytes 64 | tf_op jit(solution)/shard_map/while
  102.1 6.4 %copy-start.5 = (bf16[4,128,1,4,128]{4,3,1,0,2:T(4,128)(2,1)S(1)}, bf16[4,128,1,4,128]{4,3,1,0,2:T(4,128)(2,1)}, u32[]{:S(2)}) copy-start(bf16[4,128,1,4,128]{4,3,1,0,2:T(4,128)(2,1)} %copy-done.4) | copy-start | bytes 1572868 | tf_op jit(solution)/shard_map/while
  102.1 6.4 %copy-start.12 = (s32[4,8]{1,0:T(4,128)S(1)}, s32[4,8]{1,0:T(4,128)}, u32[]{:S(2)}) copy-start(s32[4,8]{1,0:T(4,128)} %copy-done.11) | copy-start | bytes 388 | tf_op jit(solution)/shard_map/while
  102.1 6.4 %copy-start.15 = (s32[4]{0:T(128)S(1)}, s32[4]{0:T(128)}, u32[]{:S(2)}) copy-start(s32[4]{0:T(128)} %get-tuple-element.344) | copy-start | bytes 52 | tf_op jit(solution)/shard_map/while
  119.8 5.8 %copy-start.16 = (s32[5]{0:T(128)S(1)}, s32[5]{0:T(128)}, u32[]{:S(2)}) copy-start(s32[5]{0:T(128)} %get-tuple-element.315) | copy-start | bytes 64 | tf_op jit(solution)/shard_map/while
  122.8 6.4 %copy-start.5 = (bf16[4,128,1,4,128]{4,3,1,0,2:T(4,128)(2,1)S(1)}, bf16[4,128,1,4,128]{4,3,1,0,2:T(4,128)(2,1)}, u32[]{:S(2)}) copy-start(bf16[4,128,1,4,128]{4,3,1,0,2:T(4,128)(2,1)} %copy-done.4) | copy-start | bytes 1572868 | tf_op jit(solution)/shard_map/while
  122.8 6.4 %copy-start.12 = (s32[4,8]{1,0:T(4,128)S(1)}, s32[4,8]{1,0:T(4,128)}, u32[]{:S(2)}) copy-start(s32[4,8]{1,0:T(4,128)} %copy-done.11) | copy-start | bytes 388 | tf_op jit(solution)/shard_map/while
  122.8 6.4 %copy-start.15 = (s32[4]{0:T(128)S(1)}, s32[4]{0:T(128)}, u32[]{:S(2)}) copy-start(s32[4]{0:T(128)} %get-tuple-element.344) | copy-start | bytes 52 | tf_op jit(solution)/shard_map/while
  129.2 20.9 %copy-start.1 = (bf16[4,128,1,4,128]{4,3,1,0,2:T(4,128)(2,1)S(1)}, bf16[4,128,1,4,128]{4,3,1,0,2:T(4,128)(2,1)}, u32[]{:S(2)}) copy-start(bf16[4,128,1,4,128]{4,3,1,0,2:T(4,128)(2,1)} %get-tuple-element.335) | copy-start | bytes 1572868
  132.0 26.2 %collective-permute-start.4 = (f32[2,512,128]{2,1,0:T(8,128)}, f32[2,512,128]{2,1,0:T(8,128)S(1)}, u32[]{:S(2)}, u32[]{:S(2)}) collective-permute-start(f32[2,512,128]{2,1,0:T(8,128)} %get-tuple-element.209), channel_id=1, source_target_pairs={{0,8},{8,16},{16,24},{24,32},{32,40},{40,48},{48,56},{56,64},{64,7... | collective-permute-start | bytes 1572872 | tf_op jit(solution)/shard_map/ppermute | solution.py:16
  133.9 37.5 %collective-permute-start.5 = (f32[2,512,128]{2,1,0:T(8,128)}, f32[2,512,128]{2,1,0:T(8,128)S(1)}, u32[]{:S(2)}, u32[]{:S(2)}) collective-permute-start(f32[2,512,128]{2,1,0:T(8,128)} %get-tuple-element.210), channel_id=1, source_target_pairs={{0,1016},{8,0},{16,8},{24,16},{32,24},{40,32},{48,40},{56,48},{64,... | collective-permute-start | bytes 1572872 | tf_op jit(solution)/shard_map/ppermute | solution.py:16
  140.6 30.8 %collective-permute-start.6 = (f32[2,512,128]{2,1,0:T(8,128)}, f32[2,512,128]{2,1,0:T(8,128)S(1)}, u32[]{:S(2)}, u32[]{:S(2)}) collective-permute-start(f32[2,512,128]{2,1,0:T(8,128)} %get-tuple-element.212), channel_id=1, source_target_pairs={{0,16},{8,24},{16,32},{24,40},{32,48},{40,56},{48,64},{56,72},{64,... | collective-permute-start | bytes 1572872 | tf_op jit(solution)/shard_map/ppermute | solution.py:16
  142.5 30.2 %collective-permute-start.7 = (f32[2,512,128]{2,1,0:T(8,128)S(1)}, f32[2,512,128]{2,1,0:T(8,128)S(1)}, u32[]{:S(2)}, u32[]{:S(2)}) collective-permute-start(f32[2,512,128]{2,1,0:T(8,128)S(1)} %get-tuple-element.211), channel_id=1, source_target_pairs={{0,1008},{8,1016},{16,0},{24,8},{32,16},{40,24},{48,32},{56,40},{6... | collective-permute-start | bytes 1572872 | tf_op jit(solution)/shard_map/ppermute | solution.py:16
  151.1 23.5 %all-to-all-start = ((bf16[8,64,512]{2,1,0:T(8,128)(2,1)}), bf16[8,64,512]{2,1,0:T(8,128)(2,1)S(1)}, u32[]{:S(2)}, u32[]{:S(2)}) async-start(bf16[8,64,512]{2,1,0:T(8,128)(2,1)} %all_to_all.38), calls=%async_computation | async-start | bytes 1048576 | tf_op jit(solution)/shard_map/all_to_all | solution.py:110
  174.6 12.2 %all-to-all-start.2 = ((bf16[8,64,128]{2,1,0:T(8,128)(2,1)}), bf16[8,64,128]{2,1,0:T(8,128)(2,1)S(1)}, u32[]{:S(2)}, u32[]{:S(2)}) async-start(bf16[8,64,128]{2,1,0:T(8,128)(2,1)} %bitcast.56), calls=%async_computation.2 | async-start | bytes 262144 | tf_op jit(solution)/shard_map/all_to_all | solution.py:112
  186.8 9.4 %all-to-all-start.1 = ((bf16[8,64,128]{2,1,0:T(8,128)(2,1)}), bf16[8,64,128]{2,1,0:T(8,128)(2,1)S(1)}, u32[]{:S(2)}, u32[]{:S(2)}) async-start(bf16[8,64,128]{2,1,0:T(8,128)(2,1)} %bitcast.54), calls=%async_computation.1 | async-start | bytes 262144 | tf_op jit(solution)/shard_map/all_to_all | solution.py:111
  (32 other events, 93.2 us)
where the time goes:
time: 199 us; the launch traced here: 197 us
  starting transfers between devices  66 us (33%)
  local copies, waits for them, and re-layouts  47.5 us (24%)
  other arithmetic  35.2 us (18%)
  waiting for transfers between devices  29.5 us (15%)
  matrix products  17 us (9%)
    ppermute x8, starting transfers between devices, from_behind(): return lax.ppermute(x, axis, [(i, (i + by) % size) for i in range(size)])  47.9 us
    ppermute x8, waiting for transfers between devices, from_behind(): return lax.ppermute(x, axis, [(i, (i + by) % size) for i in range(size)])  20.5 us
    scatter-add x4, other arithmetic, one_block(): gradients = gradients.at[1, slot_blocks].add(dvalue_part)  11 us
    scatter-add x4, other arithmetic, one_block(): gradients = gradients.at[0, slot_blocks].add(dkey_part)  10.9 us
    transpose x4, local copies, waits for them, and re-layouts, one_block(): jnp.einsum('hgrsc,rhgd->schd', probs_bf, orows, preferred_element_type=jn...  8.2 us
    all_to_all x1, starting transfers between devices, on_device(): lax.all_to_all(dqueries, 'head', split_axis=0, concat_axis=1, tiled=True)  7.11 us
    all_to_all x1, starting transfers between devices, on_device(): lax.all_to_all(dvalues, 'head', split_axis=0, concat_axis=1, tiled=True)  6.91 us
    another operation x9, other arithmetic  6.83 us
  transfers between devices with their start and end apart: 11, of which 6 were waited for; matrix products, arithmetic and copies ran while one was open for 4% of the time, Pallas kernels for 0%

commit v1 on v0

v1 whole, which is shorter than its diff:
```python
import functools
import math

import jax
import jax.numpy as jnp
from jax import lax
from jax.experimental import pallas as pl
from jax.experimental.pallas import tpu as pltpu
from jax.sharding import PartitionSpec as P

D = 128
BT = 128
SLOTS = 8
REACH = 2
SEGS = 2 * REACH + 1
CHUNKS = 2
MESH = pl.DeviceIdType.MESH
F32 = jnp.float32
BF16 = jnp.bfloat16


def nt(a, b):
    return lax.dot_general(a, b, (((1,), (1,)), ((), ())), preferred_element_type=F32)


def nn(a, b):
    return lax.dot_general(a, b, (((1,), (0,)), ((), ())), preferred_element_type=F32)


def tn(a, b):
    return lax.dot_general(a, b, (((0,), (0,)), ((), ())), preferred_element_type=F32)


def kernel(
    n_ctx, n_head, tok, group,
    q_ref, k_ref, v_ref, do_ref, table, live,
    dq_out, dk_out, dv_out,
    k_win, v_win, kg, st, wb, dop, invs, dvp, dkp, dq_buf,
    v_send1, v_recv1, v_send2, v_recv2, k_send1, k_recv1, k_send2, k_recv2,
    fin_v, fin_k, dq_land, dk_land, dv_land,
    win_ss, win_rs, red_ss, red_rs, ex_ss, ex_rs,
):
    nq = tok // BT
    nw = SEGS * nq
    rows = tok // n_head
    chunk = tok // CHUNKS
    cb = chunk // BT
    me = lax.axis_index("ctx")
    h = lax.axis_index("head")
    ahead = lax.rem(me + 1, n_ctx)
    behind = lax.rem(me + n_ctx - 1, n_ctx)
    to = (ahead, behind)
    scale = 1.0 / math.sqrt(D)
    c2 = scale * math.log2(math.e)

    def remote(src, dst, ss, rs, dev):
        return pltpu.make_async_remote_copy(
            src_ref=src, dst_ref=dst, send_sem=ss, recv_sem=rs, device_id=dev, device_id_type=MESH
        )

    barrier = pltpu.get_barrier_semaphore()
    for d in range(2):
        pl.semaphore_signal(barrier, inc=1, device_id={"ctx": to[d]}, device_id_type=MESH)
    for t in range(1, n_head):
        pl.semaphore_signal(
            barrier, inc=1, device_id={"head": lax.rem(h + t, n_head)}, device_id_type=MESH
        )
    pl.semaphore_wait(barrier, 2 + n_head - 1)

    near, far = (1, 3), (0, 4)

    def win(a, hop, d, c):
        ref, window = ((k_ref, k_win), (v_ref, v_win))[a]
        if hop == 0:
            src = ref.at[pl.ds(c * cb, cb)]
            seg = near[d]
        else:
            src = window.at[pl.ds(near[d] * nq + c * cb, cb)]
            seg = far[d]
        dst = window.at[pl.ds(seg * nq + c * cb, cb)]
        return remote(src, dst, win_ss.at[a, hop, d, c], win_rs.at[a, hop, d, c], {"ctx": to[d]})

    both = [(c, d) for c in range(CHUNKS) for d in range(2)]
    for c, d in both:
        win(0, 0, d, c).start()

    k_win[pl.ds(REACH * nq, nq)] = k_ref[...]
    v_win[pl.ds(REACH * nq, nq)] = v_ref[...]
    k_win[nw] = jnp.zeros((BT, D), BF16)
    v_win[nw] = jnp.zeros((BT, D), BF16)
    for qb in range(nq):
        dvp[qb, SLOTS] = jnp.zeros((BT, D), F32)
        dkp[qb, SLOTS] = jnp.zeros((BT, D), F32)

    for c, d in both:
        win(0, 0, d, c).wait_recv()
        win(0, 1, d, c).start()
    for c, d in both:
        win(1, 0, d, c).start()
    for c, d in both:
        win(0, 1, d, c).wait_recv()

    def stack_heads(ref, qb):
        r = pl.ds(pl.multiple_of(qb * BT, BT), BT)
        return jnp.concatenate([ref[r, g * D:(g + 1) * D] for g in range(group)], axis=0)

    def gather_blocks(window, first, qb):
        for s in range(SLOTS):
            kg[pl.ds(s * BT, BT), :] = window[table[qb, first + s]]

    width = group * BT

    def probs_step(qb, carry):
        for c in range(CHUNKS):
            @pl.when(qb == c + 1)
            def _():
                for d in range(2):
                    win(1, 0, d, c).wait_recv()
                    win(1, 1, d, c).start()
        qs = stack_heads(q_ref, qb)
        gather_blocks(k_win, 0, qb)
        st[...] = nt(kg[...], qs)
        top = jnp.max(st[...], axis=0, keepdims=True) * c2
        total = jnp.zeros((1, width), F32)
        for s in range(SLOTS):
            w = jnp.exp2(st[pl.ds(s * BT, BT), :] * c2 - top).astype(BF16)
            part = jnp.sum(w.astype(F32), axis=0, keepdims=True)
            total = total + part * live[qb, s]
            wb[qb, pl.ds(s * BT, BT), :] = w
        norm = 1.0 / total
        invs[qb] = jnp.broadcast_to(norm, (8, width))
        by_row = jnp.transpose(jnp.broadcast_to(norm, (D, width)))
        scaled = (stack_heads(do_ref, qb).astype(F32) * by_row).astype(BF16)
        dop[qb] = scaled
        dvp[qb, pl.ds(0, SLOTS)] = nn(wb[qb], scaled).reshape(SLOTS, BT, D)
        return carry

    lax.fori_loop(0, nq, probs_step, 0)

    def block_sum(part, w):
        acc = None
        for qb in range(nq):
            one = part[qb, table[qb, 2 * SLOTS + w]]
            acc = one if acc is None else acc + one
        return acc

    back = (behind, ahead)
    sets = (
        (dkp, scale, k_send1, k_recv1, k_send2, k_recv2, fin_k),
        (dvp, 1.0, v_send1, v_recv1, v_send2, v_recv2, fin_v),
    )

    def red(a, hop, d, c):
        src, dst = (sets[a][2], sets[a][3]) if hop == 0 else (sets[a][4], sets[a][5])
        return remote(
            src.at[d, c], dst.at[d, c],
            red_ss.at[a, hop, d, c], red_rs.at[a, hop, d, c], {"ctx": back[d]},
        )

    def red_first(a):
        part, factor, send1 = sets[a][:3]
        for c, d in both:
            for b in range(cb):
                w = far[d] * nq + c * cb + b
                send1[d, c, pl.ds(b * BT, BT), :] = (block_sum(part, w) * factor).astype(BF16)
            red(a, 0, d, c).start()

    def red_second(a, c):
        part, factor, _, recv1, send2 = sets[a][:5]
        for d in range(2):
            red(a, 0, d, c).wait_recv()
            for b in range(cb):
                w = near[d] * nq + c * cb + b
                came = recv1[d, c, pl.ds(b * BT, BT), :].astype(F32)
                send2[d, c, pl.ds(b * BT, BT), :] = (block_sum(part, w) * factor + came).astype(BF16)
            red(a, 1, d, c).start()

    def red_last(a):
        part, factor, _, _, _, recv2, fin = sets[a]
        for c in range(CHUNKS):
            for d in range(2):
                red(a, 1, d, c).wait_recv()
            for b in range(cb):
                r = pl.ds(b * BT, BT)
                own = block_sum(part, REACH * nq + c * cb + b) * factor
                whole = own + recv2[0, c, r, :].astype(F32) + recv2[1, c, r, :].astype(F32)
                fin[pl.ds(c * chunk + b * BT, BT), :] = whole.astype(BF16)

    ex_bufs = ((dq_buf, dq_land, dq_out), (fin_k, dk_land, dk_out), (fin_v, dv_land, dv_out))

    def exchange(a, t):
        src, land, _ = ex_bufs[a]
        dev = lax.rem(h + t, n_head)
        return remote(
            src.at[pl.ds(pl.multiple_of(dev * rows, rows), rows), :], land.at[h],
            ex_ss.at[a, t], ex_rs.at[a, t], {"head": dev},
        )

    def exchange_start(a):
        src, land, _ = ex_bufs[a]
        for t in range(1, n_head):
            exchange(a, t).start()
        land[h] = src[pl.ds(pl.multiple_of(h * rows, rows), rows), :]

    def exchange_end(a):
        _, land, out = ex_bufs[a]
        w = land.shape[2]
        for t in range(1, n_head):
            exchange(a, t).wait_recv()
        for j in range(n_head):
            out[:, j * w:(j + 1) * w] = land[j]

    red_first(1)
    for c, d in both:
        win(1, 1, d, c).wait_recv()

    def scores_step(qb, carry):
        for c in range(CHUNKS):
            @pl.when(qb == nq - CHUNKS + c)
            def _():
                red_second(1, c)
        gather_blocks(v_win, SLOTS, qb)
        st[...] = nt(kg[...], dop[qb])
        delta = jnp.zeros((1, width), F32)
        for s in range(SLOTS):
            r = pl.ds(s * BT, BT)
            delta = delta + jnp.sum(wb[qb, r, :].astype(F32) * st[r, :], axis=0, keepdims=True)
        delta = delta * invs[qb, 0:1, :]
        for s in range(SLOTS):
            r = pl.ds(s * BT, BT)
            wb[qb, r, :] = (wb[qb, r, :].astype(F32) * (st[r, :] - delta)).astype(BF16)
        dkp[qb, pl.ds(0, SLOTS)] = nn(wb[qb], stack_heads(q_ref, qb)).reshape(SLOTS, BT, D)
        return carry

    lax.fori_loop(0, nq, scores_step, 0)
    red_first(0)

    def queries_step(qb, carry):
        gather_blocks(k_win, SLOTS, qb)
        dq = (tn(wb[qb], kg[...]) * scale).astype(BF16)
        r = pl.ds(pl.multiple_of(qb * BT, BT), BT)
        for g in range(group):
            dq_buf[r, g * D:(g + 1) * D] = dq[g * BT:(g + 1) * BT, :]
        return carry

    lax.fori_loop(0, nq, queries_step, 0)
    exchange_start(0)
    red_last(1)
    exchange_start(2)
    for c in range(CHUNKS):
        red_second(0, c)
    exchange_end(2)
    red_last(0)
    exchange_start(1)
    exchange_end(0)
    exchange_end(1)

    for c, d in both:
        for a in range(2):
            for hop in range(2):
                win(a, hop, d, c).wait_send()
                red(a, hop, d, c).wait_send()
    for a in range(3):
        for t in range(1, n_head):
            exchange(a, t).wait_send()


def slot_tables(n_ctx, nq, nw, blocks, counts):
    first = (lax.axis_index("ctx") - REACH) * nq
    local = jnp.mod(blocks - first, n_ctx * nq)
    slots = jnp.arange(SLOTS, dtype=jnp.int32)
    live = slots[None] < counts[:, None]
    scored = jnp.where(live, local, local[:, :1])
    zeroed = jnp.where(live, local, nw)
    hit = zeroed[:, None, :] == jnp.arange(nw, dtype=jnp.int32)[None, :, None]
    slot = jnp.min(jnp.where(hit, slots[None, None], SLOTS), axis=2)
    return jnp.concatenate([scored, zeroed, slot], axis=1), live.astype(F32)


def on_device(n_ctx, n_head, queries, keys, values, output_gradient, blocks, counts):
    tok, qw = queries.shape
    group = qw // D
    nq = tok // BT
    nw = SEGS * nq
    rows = tok // n_head
    chunk = tok // CHUNKS
    vmem = pl.BlockSpec(memory_space=pltpu.VMEM)
    smem = pl.BlockSpec(memory_space=pltpu.SMEM)
    hop = pltpu.VMEM((2, CHUNKS, chunk, D), BF16)
    sems = pltpu.SemaphoreType.DMA((2, 2, 2, CHUNKS))
    width = group * BT
    return pl.pallas_call(
        functools.partial(kernel, n_ctx, n_head, tok, group),
        out_shape=(
            jax.ShapeDtypeStruct((rows, n_head * qw), BF16),
            jax.ShapeDtypeStruct((rows, n_head * D), BF16),
            jax.ShapeDtypeStruct((rows, n_head * D), BF16),
        ),
        in_specs=[vmem] * 4 + [smem] * 2,
        out_specs=(vmem,) * 3,
        scratch_shapes=[
            pltpu.VMEM((nw + 1, BT, D), BF16),
            pltpu.VMEM((nw + 1, BT, D), BF16),
            pltpu.VMEM((SLOTS * BT, D), BF16),
            pltpu.VMEM((SLOTS * BT, width), F32),
            pltpu.VMEM((nq, SLOTS * BT, width), BF16),
            pltpu.VMEM((nq, width, D), BF16),
            pltpu.VMEM((nq, 8, width), F32),
            pltpu.VMEM((nq, SLOTS + 1, BT, D), F32),
            pltpu.VMEM((nq, SLOTS + 1, BT, D), F32),
            pltpu.VMEM((tok, qw), BF16),
            hop, hop, hop, hop, hop, hop, hop, hop,
            pltpu.VMEM((tok, D), BF16),
            pltpu.VMEM((tok, D), BF16),
            pltpu.VMEM((n_head, rows, qw), BF16),
            pltpu.VMEM((n_head, rows, D), BF16),
            pltpu.VMEM((n_head, rows, D), BF16),
            sems, sems, sems, sems,
            pltpu.SemaphoreType.DMA((3, n_head)),
            pltpu.SemaphoreType.DMA((3, n_head)),
        ],
        compiler_params=pltpu.CompilerParams(
            collective_id=0, has_side_effects=True, vmem_limit_bytes=60 * 1024 * 1024
        ),
    )(
        queries, keys.reshape(nq, BT, D), values.reshape(nq, BT, D), output_gradient,
        *slot_tables(n_ctx, nq, nw, blocks, counts),
    )


def solution(mesh):
    return jax.shard_map(
        functools.partial(on_device, mesh.shape["ctx"], mesh.shape["head"]),
        mesh=mesh,
        in_specs=(
            P("ctx", "head"),
            P("ctx", "head"),
            P("ctx", "head"),
            P("ctx", "head"),
            P("ctx", None),
            P("ctx"),
        ),
        out_specs=(P(("ctx", "head"), None), P(("ctx", "head"), None), P(("ctx", "head"), None)),
        check_vma=False,
    )
```

time: 199 us -> 73.2 us (0.37)
  Pallas kernels: 0 us -> 66.5 us
  starting transfers between devices: 66 us -> 0 us
  local copies, waits for them, and re-layouts: 47.5 us -> 4.27 us
  other arithmetic: 35.2 us -> 1.54 us
  waiting for transfers between devices: 29.5 us -> 0 us
  matrix products: 17 us -> 0 us
    pallas_call x0 -> x1, Pallas kernels: none -> 66.5 us  [on_device(): pl.pallas_call(functools.partial(kernel, n_ctx, n_head, tok, group), out_...]
    ppermute x8 -> x0, starting transfers between devices: 47.9 us -> none  [from_behind(): return lax.ppermute(x, axis, [(i, (i + by) % size) for i in range(size)])]
    scatter-add x8 -> x0, other arithmetic: 21.9 us -> none  [the longest x4 11 us: one_block(): gradients = gradients.at[1, slot_blocks].add(dvalue_part)]
    ppermute x8 -> x0, waiting for transfers between devices: 20.5 us -> none  [from_behind(): return lax.ppermute(x, axis, [(i, (i + by) % size) for i in range(size)])]
    all_to_all x3 -> x0, starting transfers between devices: 18.2 us -> none  [the longest x1 7.11 us: on_device(): lax.all_to_all(dqueries, 'head', split_axis=0, concat_axis=1, tiled=True)]
    dot_general x20 -> x0, matrix products: 17 us -> none  [the longest x4 6.39 us: one_block(): jnp.einsum('hgrsc,rhgd->schd', probs_bf, orows, preferred_element_type=jn...]
    all_to_all x3 -> x0, waiting for transfers between devices: 9.06 us -> none  [the longest x1 4.62 us: on_device(): lax.all_to_all(dkeys, 'head', split_axis=0, concat_axis=1, tiled=True)]
    squeeze x5 -> x0, local copies, waits for them, and re-layouts: 8.26 us -> none  [the longest x4 5.49 us: one_block(): kblock = extended[0][slot_blocks]]
  transfers between devices with their start and end apart: 11 -> 0, of which waited for: 6 -> 0; matrix products, arithmetic and copies ran while one was open for 4% -> 0% of each run, Pallas kernels for 0% -> 0%
where the time goes in v1:
time: 73.2 us; the launch traced here: 72.9 us
  Pallas kernels  66.5 us (91%)
  local copies, waits for them, and re-layouts  4.27 us (6%)
  other arithmetic  1.54 us (2%)
    pallas_call x1, Pallas kernels, on_device(): pl.pallas_call(functools.partial(kernel, n_ctx, n_head, tok, group), out_...  66.5 us
    unnamed x11, local copies, waits for them, and re-layouts  4.16 us

profile of v1, /device:TPU:1, one launch (start us, length us, event | category | flops | bytes accessed | tf_op | source)
XLA Modules:
  0.0 72.9 jit_solution(4868673454227144798)
XLA Ops:
  0.6 0.0 copy-start.2
  0.6 0.0 copy-start.3
  0.7 0.6 copy-done.2
  1.3 0.6 fusion.1.live
  1.9 0.0 copy-done.3
  1.9 0.1 fusion.2
  2.0 0.1 slice_reduce_fusion
  2.1 0.1 fusion.3
  2.2 0.1 select_reduce_fusion
  2.3 0.7 pad_add_fusion.table
  2.9 66.5 %shard_map.85 = (bf16[64,4096]{1,0:T(8,128)(2,1)}, bf16[64,1024]{1,0:T(8,128)(2,1)}, bf16[64,1024]{1,0:T(8,128)(2,1)}) custom-call(bf16[512,512]{1,0:T(8,128)(2,1)} %q_ref.1, bf16[4,128,128]{2,1,0:T(8,128)(2,1)} %bitcast.2, bf16[4,128,128]{2,1,0:T(8,128)(2,1)} %bitcast.3, bf16[512,512]{1,0:T(8,128)(2,1)} %do_ref.1, s32[4,36]{1,0:T(4,128)} %pad_add_fusion.table, ...), custom_call_target="tpu_custom_call" | custom-call | tf_op jit(solution)/shard_map/pallas_call | solution.py:292
  69.4 0.0 copy-start.1
  69.4 1.9 %copy.12 = bf16[64,4096]{1,0:T(8,128)(2,1)} copy(bf16[64,4096]{1,0:T(8,128)(2,1)} %get-tuple-element.8) | data formatting | bytes 1048576
  71.3 0.0 copy-done.1
  71.3 0.0 copy-start
  71.3 0.7 copy.13
  72.0 0.3 copy-done
  72.3 0.7 copy.14
Async XLA Ops:
  0.6 0.7 copy-start.2
  0.6 1.3 %copy-start.3 = (s32[4,8]{1,0:T(4,128)S(1)}, s32[4,8]{1,0:T(4,128)}, u32[]{:S(2)}) copy-start(s32[4,8]{1,0:T(4,128)} %param.10) | copy-start | bytes 388
  69.4 1.9 %copy-start.1 = (bf16[64,1024]{1,0:T(8,128)(2,1)S(1)}, bf16[64,1024]{1,0:T(8,128)(2,1)}, u32[]{:S(2)}) copy-start(bf16[64,1024]{1,0:T(8,128)(2,1)} %get-tuple-element.9) | copy-start | bytes 393220
  71.3 1.0 %copy-start = (bf16[64,1024]{1,0:T(8,128)(2,1)S(1)}, bf16[64,1024]{1,0:T(8,128)(2,1)}, u32[]{:S(2)}) copy-start(bf16[64,1024]{1,0:T(8,128)(2,1)} %get-tuple-element.10) | copy-start | bytes 393220

commit v2 on v1

--- a/solution.py
+++ b/solution.py
@@ -31,14 +31,41 @@
     return lax.dot_general(a, b, (((0,), (0,)), ((), ())), preferred_element_type=F32)
 
 
+def slot_table(first, total_blocks, nq, nw, blocks, counts_ref):
+    shape = (nq, BT)
+    column = lax.broadcasted_iota(jnp.int32, shape, 1)
+    row = lax.broadcasted_iota(jnp.int32, shape, 0)
+    counts = jnp.zeros(shape, jnp.int32)
+    for qb in range(nq):
+        counts = jnp.where(row == qb, counts_ref[qb], counts)
+    local = blocks - first
+    local = jnp.where(local < 0, local + total_blocks, local)
+    local = jnp.where(local >= total_blocks, local - total_blocks, local)
+    local = jnp.clip(local, 0, nw - 1)
+    window_block = column - 2 * SLOTS
+    inside = (window_block >= 0) & (window_block < nw)
+    table = jnp.where(inside, SLOTS, 0)
+    lead = jnp.broadcast_to(local[:, :1], shape)
+    for s in range(SLOTS):
+        block = jnp.broadcast_to(local[:, s:s + 1], shape)
+        live = counts > s
+        zeroed = jnp.where(live, block, nw)
+        table = jnp.where(column == s, jnp.where(live, block, lead), table)
+        table = jnp.where(column == SLOTS + s, zeroed, table)
+        table = jnp.where(inside & (window_block == zeroed), s, table)
+        table = jnp.where(window_block == nw + s, jnp.where(live, 1, 0), table)
+    return table
+
+
 def kernel(
     n_ctx, n_head, tok, group,
-    q_ref, k_ref, v_ref, do_ref, table, live,
-    dq_out, dk_out, dv_out,
+    q_hbm, k_ref, v_ref, do_hbm, blocks_ref, counts_ref,
+    dq_land, dk_land, dv_land,
+    q_ref, do_ref, mask, table_v, table,
     k_win, v_win, kg, st, wb, dop, invs, dvp, dkp, dq_buf,
     v_send1, v_recv1, v_send2, v_recv2, k_send1, k_recv1, k_send2, k_recv2,
-    fin_v, fin_k, dq_land, dk_land, dv_land,
-    win_ss, win_rs, red_ss, red_rs, ex_ss, ex_rs,
+    fin_v, fin_k,
+    win_ss, win_rs, red_ss, red_rs, ex_ss, ex_rs, own_s,
 ):
     nq = tok // BT
     nw = SEGS * nq
@@ -58,6 +85,13 @@
             src_ref=src, dst_ref=dst, send_sem=ss, recv_sem=rs, device_id=dev, device_id_type=MESH
         )
 
+    loads = [
+        pltpu.make_async_copy(k_ref, k_win.at[pl.ds(REACH * nq, nq)], own_s.at[0]),
+        pltpu.make_async_copy(q_hbm, q_ref, own_s.at[1]),
+        pltpu.make_async_copy(do_hbm, do_ref, own_s.at[2]),
+        pltpu.make_async_copy(v_ref, v_win.at[pl.ds(REACH * nq, nq)], own_s.at[3]),
+    ]
+
     barrier = pltpu.get_barrier_semaphore()
     for d in range(2):
         pl.semaphore_signal(barrier, inc=1, device_id={"ctx": to[d]}, device_id_type=MESH)
@@ -83,9 +117,17 @@
     both = [(c, d) for c in range(CHUNKS) for d in range(2)]
     for c, d in both:
         win(0, 0, d, c).start()
-
-    k_win[pl.ds(REACH * nq, nq)] = k_ref[...]
-    v_win[pl.ds(REACH * nq, nq)] = v_ref[...]
+    for load in loads:
+        load.start()
+
+    table_v[pl.ds(0, nq), :] = slot_table(
+        (me - REACH) * nq, n_ctx * nq, nq, nw, blocks_ref[...], counts_ref
+    )
+    table_v[pl.ds(nq, 8 - nq), :] = jnp.zeros((8 - nq, BT), jnp.int32)
+    tables = pltpu.make_async_copy(table_v, table, own_s.at[7])
+    tables.start()
+    mask[0] = jnp.zeros((8, group * BT), F32)
+    mask[1] = jnp.ones((8, group * BT), F32)
     k_win[nw] = jnp.zeros((BT, D), BF16)
     v_win[nw] = jnp.zeros((BT, D), BF16)
     for qb in range(nq):
@@ -97,6 +139,9 @@
         win(0, 1, d, c).start()
     for c, d in both:
         win(1, 0, d, c).start()
+    for load in loads:
+        load.wait()
+    tables.wait()
     for c, d in both:
         win(0, 1, d, c).wait_recv()
 
@@ -121,13 +166,13 @@
         gather_blocks(k_win, 0, qb)
         st[...] = nt(kg[...], qs)
         top = jnp.max(st[...], axis=0, keepdims=True) * c2
-        total = jnp.zeros((1, width), F32)
+        total = jnp.zeros((8, width), F32)
         for s in range(SLOTS):
             w = jnp.exp2(st[pl.ds(s * BT, BT), :] * c2 - top).astype(BF16)
-            part = jnp.sum(w.astype(F32), axis=0, keepdims=True)
-            total = total + part * live[qb, s]
+            part = jnp.sum(w.astype(F32).reshape(-1, 8, width), axis=0)
+            total = total + part * mask[table[qb, 2 * SLOTS + nw + s]]
             wb[qb, pl.ds(s * BT, BT), :] = w
-        norm = 1.0 / total
+        norm = 1.0 / jnp.sum(total, axis=0, keepdims=True)
         invs[qb] = jnp.broadcast_to(norm, (8, width))
         by_row = jnp.transpose(jnp.broadcast_to(norm, (D, width)))
         scaled = (stack_heads(do_ref, qb).astype(F32) * by_row).astype(BF16)
@@ -186,29 +231,30 @@
                 whole = own + recv2[0, c, r, :].astype(F32) + recv2[1, c, r, :].astype(F32)
                 fin[pl.ds(c * chunk + b * BT, BT), :] = whole.astype(BF16)
 
-    ex_bufs = ((dq_buf, dq_land, dq_out), (fin_k, dk_land, dk_out), (fin_v, dv_land, dv_out))
+    ex_bufs = ((dq_buf, dq_land), (fin_k, dk_land), (fin_v, dv_land))
 
     def exchange(a, t):
-        src, land, _ = ex_bufs[a]
+        src, land = ex_bufs[a]
         dev = lax.rem(h + t, n_head)
         return remote(
             src.at[pl.ds(pl.multiple_of(dev * rows, rows), rows), :], land.at[h],
             ex_ss.at[a, t], ex_rs.at[a, t], {"head": dev},
         )
 
+    def own(a):
+        src, land = ex_bufs[a]
+        mine = src.at[pl.ds(pl.multiple_of(h * rows, rows), rows), :]
+        return pltpu.make_async_copy(mine, land.at[h], own_s.at[4 + a])
+
     def exchange_start(a):
-        src, land, _ = ex_bufs[a]
         for t in range(1, n_head):
             exchange(a, t).start()
-        land[h] = src[pl.ds(pl.multiple_of(h * rows, rows), rows), :]
+        own(a).start()
 
     def exchange_end(a):
-        _, land, out = ex_bufs[a]
-        w = land.shape[2]
+        own(a).wait()
         for t in range(1, n_head):
             exchange(a, t).wait_recv()
-        for j in range(n_head):
-            out[:, j * w:(j + 1) * w] = land[j]
 
     red_first(1)
     for c, d in both:
@@ -249,9 +295,9 @@
     exchange_start(2)
     for c in range(CHUNKS):
         red_second(0, c)
-    exchange_end(2)
     red_last(0)
     exchange_start(1)
+    exchange_end(2)
     exchange_end(0)
     exchange_end(1)
 
@@ -265,16 +311,11 @@
             exchange(a, t).wait_send()
 
 
-def slot_tables(n_ctx, nq, nw, blocks, counts):
-    first = (lax.axis_index("ctx") - REACH) * nq
-    local = jnp.mod(blocks - first, n_ctx * nq)
-    slots = jnp.arange(SLOTS, dtype=jnp.int32)
-    live = slots[None] < counts[:, None]
-    scored = jnp.where(live, local, local[:, :1])
-    zeroed = jnp.where(live, local, nw)
-    hit = zeroed[:, None, :] == jnp.arange(nw, dtype=jnp.int32)[None, :, None]
-    slot = jnp.min(jnp.where(hit, slots[None, None], SLOTS), axis=2)
-    return jnp.concatenate([scored, zeroed, slot], axis=1), live.astype(F32)
+def assemble(dq_land, dk_land, dv_land, dq_out, dk_out, dv_out):
+    for land, out in ((dq_land, dq_out), (dk_land, dk_out), (dv_land, dv_out)):
+        parts, _, w = land.shape
+        for j in range(parts):
+            out[:, j * w:(j + 1) * w] = land[j]
 
 
 def on_device(n_ctx, n_head, queries, keys, values, output_gradient, blocks, counts):
@@ -289,16 +330,22 @@
     hop = pltpu.VMEM((2, CHUNKS, chunk, D), BF16)
     sems = pltpu.SemaphoreType.DMA((2, 2, 2, CHUNKS))
     width = group * BT
-    return pl.pallas_call(
+    hbm = pl.BlockSpec(memory_space=pl.ANY)
+    landed = pl.pallas_call(
         functools.partial(kernel, n_ctx, n_head, tok, group),
         out_shape=(
-            jax.ShapeDtypeStruct((rows, n_head * qw), BF16),
-            jax.ShapeDtypeStruct((rows, n_head * D), BF16),
-            jax.ShapeDtypeStruct((rows, n_head * D), BF16),
+            jax.ShapeDtypeStruct((n_head, rows, qw), BF16),
+            jax.ShapeDtypeStruct((n_head, rows, D), BF16),
+            jax.ShapeDtypeStruct((n_head, rows, D), BF16),
         ),
-        in_specs=[vmem] * 4 + [smem] * 2,
-        out_specs=(vmem,) * 3,
+        in_specs=[hbm] * 4 + [vmem, smem],
+        out_specs=(hbm,) * 3,
         scratch_shapes=[
+            pltpu.VMEM((tok, qw), BF16),
+            pltpu.VMEM((tok, qw), BF16),
+            pltpu.VMEM((2, 8, width), F32),
+            pltpu.VMEM((8, BT), jnp.int32),
+            pltpu.SMEM((8, BT), jnp.int32),
             pltpu.VMEM((nw + 1, BT, D), BF16),
             pltpu.VMEM((nw + 1, BT, D), BF16),
             pltpu.VMEM((SLOTS * BT, D), BF16),
@@ -312,20 +359,27 @@
             hop, hop, hop, hop, hop, hop, hop, hop,
             pltpu.VMEM((tok, D), BF16),
             pltpu.VMEM((tok, D), BF16),
-            pltpu.VMEM((n_head, rows, qw), BF16),
-            pltpu.VMEM((n_head, rows, D), BF16),
-            pltpu.VMEM((n_head, rows, D), BF16),
             sems, sems, sems, sems,
             pltpu.SemaphoreType.DMA((3, n_head)),
             pltpu.SemaphoreType.DMA((3, n_head)),
+            pltpu.SemaphoreType.DMA((8,)),
         ],
         compiler_params=pltpu.CompilerParams(
             collective_id=0, has_side_effects=True, vmem_limit_bytes=60 * 1024 * 1024
         ),
     )(
-        queries, keys.reshape(nq, BT, D), values.reshape(nq, BT, D), output_gradient,
-        *slot_tables(n_ctx, nq, nw, blocks, counts),
+        queries, keys.reshape(nq, BT, D), values.reshape(nq, BT, D), output_gradient, blocks, counts
     )
+    return pl.pallas_call(
+        assemble,
+        out_shape=(
+            jax.ShapeDtypeStruct((rows, n_head * qw), BF16),
+            jax.ShapeDtypeStruct((rows, n_head * D), BF16),
+            jax.ShapeDtypeStruct((rows, n_head * D), BF16),
+        ),
+        in_specs=[vmem] * 3,
+        out_specs=(vmem,) * 3,
+    )(*landed)
 
 
 def solution(mesh):

time: 73.2 us -> 68.3 us (0.933)
  local copies, waits for them, and re-layouts: 4.27 us -> 0 us
  other arithmetic: 1.54 us -> 0 us
  Pallas kernels: 66.5 us -> 67.5 us
    unnamed x11 -> x0, local copies, waits for them, and re-layouts: 4.16 us -> none
    pallas_call x0 -> x1, Pallas kernels: none -> 2.04 us  [on_device(): pl.pallas_call(assemble, out_shape=(jax.ShapeDtypeStruct((rows, n_head *...]
    pallas_call x1, Pallas kernels: 66.5 us -> 65.4 us  [on_device(): pl.pallas_call(functools.partial(kernel, n_ctx, n_head, tok, group), out_...]
where the time goes in v2:
time: 68.3 us; the launch traced here: 68.1 us
  Pallas kernels  67.5 us (99%)
    pallas_call x1, Pallas kernels, on_device(): pl.pallas_call(functools.partial(kernel, n_ctx, n_head, tok, group), out_...  65.4 us
    pallas_call x1, Pallas kernels, on_device(): pl.pallas_call(assemble, out_shape=(jax.ShapeDtypeStruct((rows, n_head *...  2.04 us

profile of v2, /device:TPU:1, one launch (start us, length us, event | category | flops | bytes accessed | tf_op | source)
XLA Modules:
  0.0 68.1 jit_solution(18380448468744376506)
XLA Ops:
  0.6 65.4 %shard_map.85 = (bf16[8,64,512]{2,1,0:T(8,128)(2,1)}, bf16[8,64,128]{2,1,0:T(8,128)(2,1)}, bf16[8,64,128]{2,1,0:T(8,128)(2,1)}) custom-call(bf16[512,512]{1,0:T(8,128)(2,1)} %q_hbm.1, bf16[4,128,128]{2,1,0:T(8,128)(2,1)} %bitcast.2, bf16[4,128,128]{2,1,0:T(8,128)(2,1)} %bitcast.3, bf16[512,512]{1,0:T(8,128)(2,1)} %do_hbm.1, s32[4,8]{1,0:T(4,128)} %blocks_ref.1, ...), custom_call_target="tpu_custom_call" | custom-call | tf_op jit(solution)/shard_map/pallas_call | solution.py:334
  66.1 2.0 %shard_map.86 = (bf16[64,4096]{1,0:T(8,128)(2,1)}, bf16[64,1024]{1,0:T(8,128)(2,1)}, bf16[64,1024]{1,0:T(8,128)(2,1)}) custom-call(bf16[8,64,512]{2,1,0:T(8,128)(2,1)} %get-tuple-element.6.dq_land, bf16[8,64,128]{2,1,0:T(8,128)(2,1)} %get-tuple-element.7.dk_land, bf16[8,64,128]{2,1,0:T(8,128)(2,1)} %get-tuple-element.8.dv_land), custom_call_target="tpu_custom_call" | custom-call | tf_op jit(solution)/shard_map/pallas_call | solution.py:373

commit v3 on v2

--- a/solution.py
+++ b/solution.py
@@ -14,6 +14,7 @@
 REACH = 2
 SEGS = 2 * REACH + 1
 CHUNKS = 2
+UNROLL = 8
 MESH = pl.DeviceIdType.MESH
 F32 = jnp.float32
 BF16 = jnp.bfloat16
@@ -65,10 +66,11 @@
     k_win, v_win, kg, st, wb, dop, invs, dvp, dkp, dq_buf,
     v_send1, v_recv1, v_send2, v_recv2, k_send1, k_recv1, k_send2, k_recv2,
     fin_v, fin_k,
-    win_ss, win_rs, red_ss, red_rs, ex_ss, ex_rs, own_s,
+    win_ss, win_rs, red_ss, red_rs, ex_ss, ex_rs, own_s, head_s,
 ):
     nq = tok // BT
     nw = SEGS * nq
+    width = group * BT
     rows = tok // n_head
     chunk = tok // CHUNKS
     cb = chunk // BT
@@ -87,10 +89,12 @@
 
     loads = [
         pltpu.make_async_copy(k_ref, k_win.at[pl.ds(REACH * nq, nq)], own_s.at[0]),
-        pltpu.make_async_copy(q_hbm, q_ref, own_s.at[1]),
-        pltpu.make_async_copy(do_hbm, do_ref, own_s.at[2]),
-        pltpu.make_async_copy(v_ref, v_win.at[pl.ds(REACH * nq, nq)], own_s.at[3]),
+        pltpu.make_async_copy(v_ref, v_win.at[pl.ds(REACH * nq, nq)], own_s.at[1]),
     ]
+    for g in range(group):
+        cols = pl.ds(g * D, D)
+        loads.append(pltpu.make_async_copy(q_hbm.at[:, :, cols], q_ref.at[:, g], head_s.at[0, g]))
+        loads.append(pltpu.make_async_copy(do_hbm.at[:, :, cols], do_ref.at[:, g], head_s.at[1, g]))
 
     barrier = pltpu.get_barrier_semaphore()
     for d in range(2):
@@ -145,42 +149,54 @@
     for c, d in both:
         win(0, 1, d, c).wait_recv()
 
-    def stack_heads(ref, qb):
-        r = pl.ds(pl.multiple_of(qb * BT, BT), BT)
-        return jnp.concatenate([ref[r, g * D:(g + 1) * D] for g in range(group)], axis=0)
+    def stacked(ref, qb):
+        return ref[qb].reshape(width, D)
+
+    def fold(x):
+        return x.reshape(-1, 8, width)
 
     def gather_blocks(window, first, qb):
         for s in range(SLOTS):
             kg[pl.ds(s * BT, BT), :] = window[table[qb, first + s]]
 
-    width = group * BT
-
-    def probs_step(qb, carry):
+    top = None
+    for t in range(nq + 2):
         for c in range(CHUNKS):
-            @pl.when(qb == c + 1)
-            def _():
+            if t == 2 * c + 3:
                 for d in range(2):
                     win(1, 0, d, c).wait_recv()
                     win(1, 1, d, c).start()
-        qs = stack_heads(q_ref, qb)
-        gather_blocks(k_win, 0, qb)
-        st[...] = nt(kg[...], qs)
-        top = jnp.max(st[...], axis=0, keepdims=True) * c2
-        total = jnp.zeros((8, width), F32)
-        for s in range(SLOTS):
-            w = jnp.exp2(st[pl.ds(s * BT, BT), :] * c2 - top).astype(BF16)
-            part = jnp.sum(w.astype(F32).reshape(-1, 8, width), axis=0)
-            total = total + part * mask[table[qb, 2 * SLOTS + nw + s]]
-            wb[qb, pl.ds(s * BT, BT), :] = w
-        norm = 1.0 / jnp.sum(total, axis=0, keepdims=True)
-        invs[qb] = jnp.broadcast_to(norm, (8, width))
-        by_row = jnp.transpose(jnp.broadcast_to(norm, (D, width)))
-        scaled = (stack_heads(do_ref, qb).astype(F32) * by_row).astype(BF16)
-        dop[qb] = scaled
-        dvp[qb, pl.ds(0, SLOTS)] = nn(wb[qb], scaled).reshape(SLOTS, BT, D)
-        return carry
-
-    lax.fori_loop(0, nq, probs_step, 0)
+
+        def probs_step(i, carry, t=t, top=top):
+            tops, total = carry
+            group_of = pl.ds(i * UNROLL, UNROLL)
+            if t < nq:
+                blocks = [k_win[table[t, i * UNROLL + u]] for u in range(UNROLL)]
+                tile = nt(jnp.concatenate(blocks, axis=0), stacked(q_ref, t))
+                st[t % 2, group_of] = tile.reshape(UNROLL, BT, width)
+                tops = jnp.maximum(tops, jnp.max(fold(tile), axis=0))
+            if 1 <= t <= nq:
+                for u in range(UNROLL):
+                    s = i * UNROLL + u
+                    w = jnp.exp2(fold(st[(t - 1) % 2, s]) * c2 - top[None])
+                    w = w.reshape(BT, width).astype(BF16)
+                    alive = mask[table[t - 1, 2 * SLOTS + nw + s]]
+                    total = total + jnp.sum(fold(w.astype(F32)), axis=0) * alive
+                    wb[t - 1, s] = w
+            if t >= 2:
+                tile = nn(wb[t - 2, group_of].reshape(UNROLL * BT, width), dop[t - 2])
+                dvp[t - 2, group_of] = tile.reshape(UNROLL, BT, D)
+            return tops, total
+
+        start = (jnp.full((8, width), -jnp.inf, F32), jnp.zeros((8, width), F32))
+        tops, total = lax.fori_loop(0, SLOTS // UNROLL, probs_step, start)
+        if t < nq:
+            top = jnp.broadcast_to(jnp.max(tops, axis=0, keepdims=True) * c2, (8, width))
+        if 1 <= t <= nq:
+            norm = 1.0 / jnp.sum(total, axis=0, keepdims=True)
+            invs[t - 1] = jnp.broadcast_to(norm, (8, width))
+            by_row = jnp.transpose(jnp.broadcast_to(norm, (D, width)))
+            dop[t - 1] = (stacked(do_ref, t - 1).astype(F32) * by_row).astype(BF16)
 
     def block_sum(part, w):
         acc = None
@@ -260,30 +276,41 @@
     for c, d in both:
         win(1, 1, d, c).wait_recv()
 
-    def scores_step(qb, carry):
+    shift = None
+    for t in range(nq + 2):
         for c in range(CHUNKS):
-            @pl.when(qb == nq - CHUNKS + c)
-            def _():
+            if t == 2 * c + 3:
                 red_second(1, c)
-        gather_blocks(v_win, SLOTS, qb)
-        st[...] = nt(kg[...], dop[qb])
-        delta = jnp.zeros((1, width), F32)
-        for s in range(SLOTS):
-            r = pl.ds(s * BT, BT)
-            delta = delta + jnp.sum(wb[qb, r, :].astype(F32) * st[r, :], axis=0, keepdims=True)
-        delta = delta * invs[qb, 0:1, :]
-        for s in range(SLOTS):
-            r = pl.ds(s * BT, BT)
-            wb[qb, r, :] = (wb[qb, r, :].astype(F32) * (st[r, :] - delta)).astype(BF16)
-        dkp[qb, pl.ds(0, SLOTS)] = nn(wb[qb], stack_heads(q_ref, qb)).reshape(SLOTS, BT, D)
-        return carry
-
-    lax.fori_loop(0, nq, scores_step, 0)
+
+        def scores_step(i, delta, t=t, shift=shift):
+            group_of = pl.ds(i * UNROLL, UNROLL)
+            if t < nq:
+                blocks = [v_win[table[t, SLOTS + i * UNROLL + u]] for u in range(UNROLL)]
+                tile = nt(jnp.concatenate(blocks, axis=0), dop[t])
+                st[t % 2, group_of] = tile.reshape(UNROLL, BT, width)
+                weights = wb[t, group_of].reshape(UNROLL * BT, width)
+                delta = delta + jnp.sum(fold(weights.astype(F32) * tile), axis=0)
+            if 1 <= t <= nq:
+                for u in range(UNROLL):
+                    s = i * UNROLL + u
+                    centred = fold(st[(t - 1) % 2, s]) - shift[None]
+                    ds = fold(wb[t - 1, s].astype(F32)) * centred
+                    wb[t - 1, s] = ds.reshape(BT, width).astype(BF16)
+            if t >= 2:
+                tile = nn(wb[t - 2, group_of].reshape(UNROLL * BT, width), stacked(q_ref, t - 2))
+                dkp[t - 2, group_of] = tile.reshape(UNROLL, BT, D)
+            return delta
+
+        delta = lax.fori_loop(0, SLOTS // UNROLL, scores_step, jnp.zeros((8, width), F32))
+        if t < nq:
+            whole = jnp.sum(delta, axis=0, keepdims=True) * invs[t, 0:1, :]
+            shift = jnp.broadcast_to(whole, (8, width))
+
     red_first(0)
 
     def queries_step(qb, carry):
         gather_blocks(k_win, SLOTS, qb)
-        dq = (tn(wb[qb], kg[...]) * scale).astype(BF16)
+        dq = (tn(wb[qb].reshape(SLOTS * BT, width), kg[...]) * scale).astype(BF16)
         r = pl.ds(pl.multiple_of(qb * BT, BT), BT)
         for g in range(group):
             dq_buf[r, g * D:(g + 1) * D] = dq[g * BT:(g + 1) * BT, :]
@@ -341,16 +368,16 @@
         in_specs=[hbm] * 4 + [vmem, smem],
         out_specs=(hbm,) * 3,
         scratch_shapes=[
-            pltpu.VMEM((tok, qw), BF16),
-            pltpu.VMEM((tok, qw), BF16),
+            pltpu.VMEM((nq, group, BT, D), BF16),
+            pltpu.VMEM((nq, group, BT, D), BF16),
             pltpu.VMEM((2, 8, width), F32),
             pltpu.VMEM((8, BT), jnp.int32),
             pltpu.SMEM((8, BT), jnp.int32),
             pltpu.VMEM((nw + 1, BT, D), BF16),
             pltpu.VMEM((nw + 1, BT, D), BF16),
             pltpu.VMEM((SLOTS * BT, D), BF16),
-            pltpu.VMEM((SLOTS * BT, width), F32),
-            pltpu.VMEM((nq, SLOTS * BT, width), BF16),
+            pltpu.VMEM((2, SLOTS, BT, width), F32),
+            pltpu.VMEM((nq, SLOTS, BT, width), BF16),
             pltpu.VMEM((nq, width, D), BF16),
             pltpu.VMEM((nq, 8, width), F32),
             pltpu.VMEM((nq, SLOTS + 1, BT, D), F32),
@@ -363,12 +390,14 @@
             pltpu.SemaphoreType.DMA((3, n_head)),
             pltpu.SemaphoreType.DMA((3, n_head)),
             pltpu.SemaphoreType.DMA((8,)),
+            pltpu.SemaphoreType.DMA((2, group)),
         ],
         compiler_params=pltpu.CompilerParams(
             collective_id=0, has_side_effects=True, vmem_limit_bytes=60 * 1024 * 1024
         ),
     )(
-        queries, keys.reshape(nq, BT, D), values.reshape(nq, BT, D), output_gradient, blocks, counts
+        queries.reshape(nq, BT, qw), keys.reshape(nq, BT, D), values.reshape(nq, BT, D),
+        output_gradient.reshape(nq, BT, qw), blocks, counts,
     )
     return pl.pallas_call(
         assemble,

time: 68.3 us -> 68.1 us (level)
  no operation moved by 1% of the time
where the time goes in v3:
time: 68.1 us; the launch traced here: 67.9 us
  Pallas kernels  67.3 us (99%)
    pallas_call x1, Pallas kernels, on_device(): pl.pallas_call(functools.partial(kernel, n_ctx, n_head, tok, group), out_...  65.2 us
    pallas_call x1, Pallas kernels, on_device(): pl.pallas_call(assemble, out_shape=(jax.ShapeDtypeStruct((rows, n_head *...  2.04 us

profile of v3, /device:TPU:1, one launch (start us, length us, event | category | flops | bytes accessed | tf_op | source)
XLA Modules:
  0.0 67.9 jit_solution(40733948831179079)
XLA Ops:
  0.6 65.2 %shard_map.85 = (bf16[8,64,512]{2,1,0:T(8,128)(2,1)}, bf16[8,64,128]{2,1,0:T(8,128)(2,1)}, bf16[8,64,128]{2,1,0:T(8,128)(2,1)}) custom-call(bf16[4,128,512]{2,1,0:T(8,128)(2,1)} %bitcast.4, bf16[4,128,128]{2,1,0:T(8,128)(2,1)} %bitcast.6, bf16[4,128,128]{2,1,0:T(8,128)(2,1)} %bitcast.7, bf16[4,128,512]{2,1,0:T(8,128)(2,1)} %bitcast.5, s32[4,8]{1,0:T(4,128)} %blocks_ref.1, ...), custom_call_target="tpu_custom_call" | custom-call | tf_op jit(solution)/shard_map/pallas_call | solution.py:361
  65.9 2.0 %shard_map.86 = (bf16[64,4096]{1,0:T(8,128)(2,1)}, bf16[64,1024]{1,0:T(8,128)(2,1)}, bf16[64,1024]{1,0:T(8,128)(2,1)}) custom-call(bf16[8,64,512]{2,1,0:T(8,128)(2,1)} %get-tuple-element.6.dq_land, bf16[8,64,128]{2,1,0:T(8,128)(2,1)} %get-tuple-element.7.dk_land, bf16[8,64,128]{2,1,0:T(8,128)(2,1)} %get-tuple-element.8.dv_land), custom_call_target="tpu_custom_call" | custom-call | tf_op jit(solution)/shard_map/pallas_call | solution.py:402

commit v4 on v3

--- a/solution.py
+++ b/solution.py
@@ -63,7 +63,7 @@
     q_hbm, k_ref, v_ref, do_hbm, blocks_ref, counts_ref,
     dq_land, dk_land, dv_land,
     q_ref, do_ref, mask, table_v, table,
-    k_win, v_win, kg, st, wb, dop, invs, dvp, dkp, dq_buf,
+    k_win, v_win, st, wb, dop, invs, dvp, dkp, dq_buf,
     v_send1, v_recv1, v_send2, v_recv2, k_send1, k_recv1, k_send2, k_recv2,
     fin_v, fin_k,
     win_ss, win_rs, red_ss, red_rs, ex_ss, ex_rs, own_s, head_s,
@@ -155,14 +155,10 @@
     def fold(x):
         return x.reshape(-1, 8, width)
 
-    def gather_blocks(window, first, qb):
-        for s in range(SLOTS):
-            kg[pl.ds(s * BT, BT), :] = window[table[qb, first + s]]
-
     top = None
     for t in range(nq + 2):
         for c in range(CHUNKS):
-            if t == 2 * c + 3:
+            if t == 2 * c + 2:
                 for d in range(2):
                     win(1, 0, d, c).wait_recv()
                     win(1, 1, d, c).start()
@@ -279,7 +275,7 @@
     shift = None
     for t in range(nq + 2):
         for c in range(CHUNKS):
-            if t == 2 * c + 3:
+            if t == c + 3:
                 red_second(1, c)
 
         def scores_step(i, delta, t=t, shift=shift):
@@ -299,6 +295,12 @@
             if t >= 2:
                 tile = nn(wb[t - 2, group_of].reshape(UNROLL * BT, width), stacked(q_ref, t - 2))
                 dkp[t - 2, group_of] = tile.reshape(UNROLL, BT, D)
+                blocks = [k_win[table[t - 2, SLOTS + s]] for s in range(SLOTS)]
+                terms = wb[t - 2].reshape(SLOTS * BT, width)
+                dq = (tn(terms, jnp.concatenate(blocks, axis=0)) * scale).astype(BF16)
+                for g in range(group):
+                    rows_of = pl.ds((t - 2) * BT, BT)
+                    dq_buf[rows_of, g * D:(g + 1) * D] = dq[g * BT:(g + 1) * BT, :]
             return delta
 
         delta = lax.fori_loop(0, SLOTS // UNROLL, scores_step, jnp.zeros((8, width), F32))
@@ -306,18 +308,8 @@
             whole = jnp.sum(delta, axis=0, keepdims=True) * invs[t, 0:1, :]
             shift = jnp.broadcast_to(whole, (8, width))
 
+    exchange_start(0)
     red_first(0)
-
-    def queries_step(qb, carry):
-        gather_blocks(k_win, SLOTS, qb)
-        dq = (tn(wb[qb].reshape(SLOTS * BT, width), kg[...]) * scale).astype(BF16)
-        r = pl.ds(pl.multiple_of(qb * BT, BT), BT)
-        for g in range(group):
-            dq_buf[r, g * D:(g + 1) * D] = dq[g * BT:(g + 1) * BT, :]
-        return carry
-
-    lax.fori_loop(0, nq, queries_step, 0)
-    exchange_start(0)
     red_last(1)
     exchange_start(2)
     for c in range(CHUNKS):
@@ -375,7 +367,6 @@
             pltpu.SMEM((8, BT), jnp.int32),
             pltpu.VMEM((nw + 1, BT, D), BF16),
             pltpu.VMEM((nw + 1, BT, D), BF16),
-            pltpu.VMEM((SLOTS * BT, D), BF16),
             pltpu.VMEM((2, SLOTS, BT, width), F32),
             pltpu.VMEM((nq, SLOTS, BT, width), BF16),
             pltpu.VMEM((nq, width, D), BF16),

time: 68.1 us -> 68.3 us (level)
  no operation moved by 1% of the time
where the time goes in v4:
time: 68.3 us; the launch traced here: 68.1 us
  Pallas kernels  67.5 us (99%)
    pallas_call x1, Pallas kernels, on_device(): pl.pallas_call(functools.partial(kernel, n_ctx, n_head, tok, group), out_...  65.5 us
    pallas_call x1, Pallas kernels, on_device(): pl.pallas_call(assemble, out_shape=(jax.ShapeDtypeStruct((rows, n_head *...  2.04 us

profile of v4, /device:TPU:1, one launch (start us, length us, event | category | flops | bytes accessed | tf_op | source)
XLA Modules:
  0.0 68.1 jit_solution(9441782372428013970)
XLA Ops:
  0.6 65.5 %shard_map.85 = (bf16[8,64,512]{2,1,0:T(8,128)(2,1)}, bf16[8,64,128]{2,1,0:T(8,128)(2,1)}, bf16[8,64,128]{2,1,0:T(8,128)(2,1)}) custom-call(bf16[4,128,512]{2,1,0:T(8,128)(2,1)} %bitcast.4, bf16[4,128,128]{2,1,0:T(8,128)(2,1)} %bitcast.6, bf16[4,128,128]{2,1,0:T(8,128)(2,1)} %bitcast.7, bf16[4,128,512]{2,1,0:T(8,128)(2,1)} %bitcast.5, s32[4,8]{1,0:T(4,128)} %blocks_ref.1, ...), custom_call_target="tpu_custom_call" | custom-call | tf_op jit(solution)/shard_map/pallas_call | solution.py:353
  66.1 2.0 %shard_map.86 = (bf16[64,4096]{1,0:T(8,128)(2,1)}, bf16[64,1024]{1,0:T(8,128)(2,1)}, bf16[64,1024]{1,0:T(8,128)(2,1)}) custom-call(bf16[8,64,512]{2,1,0:T(8,128)(2,1)} %get-tuple-element.6.dq_land, bf16[8,64,128]{2,1,0:T(8,128)(2,1)} %get-tuple-element.7.dk_land, bf16[8,64,128]{2,1,0:T(8,128)(2,1)} %get-tuple-element.8.dv_land), custom_call_target="tpu_custom_call" | custom-call | tf_op jit(solution)/shard_map/pallas_call | solution.py:393
